TPU v7x, 32 devices: a whole 2x2x4 slice. The times are simulated.
32 devices in a mesh: batch: 8 (over z, y), mp: 4 (over x, core).
Axes of the slice: x: 2, y: 2, z: 4, core: 2. Of those that a mesh axis runs over, the one named last changes fastest.
Arguments:
- lookup_ids: int32 [64, 16384], P('batch'), may hold values from 0 to 8191
- table_feature: int32 [64], replicated, may hold values from 0 to 63, each once
- tables: bfloat16 [64, 8192, 128], P('batch'), may hold values from -6 to 6
- cross_down: bfloat16 [2, 8192, 512], P(None, 'mp'), may hold values from -0.0625 to 0.0625
- cross_up: bfloat16 [2, 512, 8192], P(None, None, 'mp'), may hold values from -0.25 to 0.25
- cross_bias: float32 [2, 8192], P(None, 'mp'), may hold values from -3 to 3
Outputs:
- crossed: bfloat16 [16384, 8192], P('batch', 'mp')
Inputs may be any that keep to these rules, and one draw needn't show every extreme that they name: `table_feature`: each number appears once.
All inputs are finite; a program needn't handle non-finite values.
Results may differ from a plain program's by a relative error of at most 0.015.
Values may be sent and summed in bfloat16 or wider, within the bound.
A program may use at most 128 MiB of HBM per device.

v0:
```python
import functools

import jax
import jax.numpy as jnp
from jax import lax
from jax.experimental import pallas as pl
from jax.experimental.pallas import tpu as pltpu
from jax.sharding import PartitionSpec as P

MESH = pl.DeviceIdType.MESH
GROUP = 16


def gather_kernel(ids_ref, table_ref, out_ref, wide, rows):
    sources, groups, _, emb_local, share = out_ref.shape
    slot = pl.program_id(0)
    buckets = wide.shape[0]
    step = 256

    @pl.loop(0, buckets // step)
    def _(i):
        part = pl.ds(pl.multiple_of(i * step, step), step)
        wide[part, :] = table_ref[0, part, :].astype(jnp.float32)

    unroll = 32

    @pl.loop(0, sources)
    def _(dest):
        @pl.loop(0, share // unroll)
        def _(i):
            base = pl.multiple_of(i * unroll, unroll)
            first = (slot * sources + dest) * share + base
            for k in range(unroll):
                at = ids_ref[first + k]
                rows[pl.ds(base + k, 1), :] = wide[pl.ds(at, 1), :]

        turned = rows[...].T.astype(jnp.bfloat16)
        for m in range(groups):
            out_ref[dest, m, 0] = turned[m * emb_local : (m + 1) * emb_local]


def gather(wanted, tables, sources, groups, share):
    slots, buckets, emb = tables.shape
    emb_local = emb // groups
    return pl.pallas_call(
        gather_kernel,
        out_shape=jax.ShapeDtypeStruct((sources, groups, slots, emb_local, share), tables.dtype),
        grid_spec=pltpu.PrefetchScalarGridSpec(
            num_scalar_prefetch=1,
            grid=(slots,),
            in_specs=[pl.BlockSpec((1, buckets, emb), lambda s, ids: (s, 0, 0))],
            out_specs=pl.BlockSpec(
                (sources, groups, 1, emb_local, share), lambda s, ids: (0, 0, s, 0, 0)
            ),
            scratch_shapes=[
                pltpu.VMEM((buckets, emb), jnp.float32),
                pltpu.VMEM((share, emb), jnp.float32),
            ],
        ),
        compiler_params=pltpu.CompilerParams(vmem_limit_bytes=40 * 2**20),
        name="lookup",
    )(wanted, tables)


def partner(me, mask, size):
    other = me
    bit = 1
    while bit < size:
        if mask & bit:
            other = other + bit * (1 - 2 * ((me // bit) % 2))
        bit *= 2
    return other


def exchange_kernel(sources, groups, src_ref, dst_ref, send_sem, recv_sem, own_sem):
    b, m = lax.axis_index("batch"), lax.axis_index("mp")
    masks = [
        (x, y)
        for x in range(sources - 1, -1, -1)
        for y in range(groups - 1, -1, -1)
        if (x, y) != (0, 0)
    ]
    peers = [(partner(b, x, sources), partner(m, y, groups)) for x, y in masks]
    barrier = pltpu.get_barrier_semaphore()
    for peer in peers:
        pl.semaphore_signal(barrier, inc=1, device_id=peer, device_id_type=MESH)
    pl.semaphore_wait(barrier, len(peers))
    copies = []
    for k, peer in enumerate(peers):
        copy = pltpu.make_async_remote_copy(
            src_ref=src_ref.at[peer[0], peer[1]],
            dst_ref=dst_ref.at[b, m],
            send_sem=send_sem.at[k],
            recv_sem=recv_sem.at[k],
            device_id=peer,
            device_id_type=MESH,
        )
        copy.start()
        copies.append(copy)
    own = pltpu.make_async_copy(src_ref.at[b, m], dst_ref.at[b, m], own_sem)
    own.start()
    own.wait()
    for copy in copies:
        copy.wait()


def exchange(sent):
    sources, groups = sent.shape[:2]
    peers = sources * groups - 1
    return pl.pallas_call(
        functools.partial(exchange_kernel, sources, groups),
        out_shape=jax.ShapeDtypeStruct(sent.shape, sent.dtype),
        in_specs=[pl.BlockSpec(memory_space=pl.ANY)],
        out_specs=pl.BlockSpec(memory_space=pl.ANY),
        scratch_shapes=[
            pltpu.SemaphoreType.DMA((peers,)),
            pltpu.SemaphoreType.DMA((peers,)),
            pltpu.SemaphoreType.DMA,
        ],
        compiler_params=pltpu.CompilerParams(collective_id=0, has_side_effects=True),
        name="exchange",
    )(sent)


def place_kernel(x_ref, column_ref, down_ref, emb_ref, term_ref, placing_ref, total):
    sources, _, slots, group, share = x_ref.shape
    i, j = pl.program_id(0), pl.program_id(1)

    @pl.when((i == 0) & (j == 0))
    def _():
        columns = lax.broadcasted_iota(jnp.int32, placing_ref.shape, 1)
        placing_ref[...] = jnp.where(column_ref[...] == columns, 1.0, 0.0).astype(jnp.bfloat16)

    x = x_ref[...].reshape(sources * slots * group, share)
    emb = lax.dot_general(
        x, placing_ref[...], (((0,), (0,)), ((), ())), preferred_element_type=jnp.float32
    ).astype(jnp.bfloat16)
    emb_ref[...] = emb
    part = jnp.dot(emb, down_ref[0], preferred_element_type=jnp.float32)

    @pl.when(j == 0)
    def _():
        total[...] = part

    @pl.when(j > 0)
    def _():
        total[...] += part

    @pl.when(j == pl.num_programs(1) - 1)
    def _():
        term_ref[...] = total[...].astype(jnp.bfloat16)


def place(received, column, cross_down):
    sources, groups, slots, emb_local, share = received.shape
    _, width, rank = cross_down.shape
    cols = sources * slots * GROUP
    return pl.pallas_call(
        place_kernel,
        out_shape=(
            jax.ShapeDtypeStruct((groups * share, width), jnp.bfloat16),
            jax.ShapeDtypeStruct((groups * share, rank), jnp.bfloat16),
        ),
        grid=(groups, emb_local // GROUP),
        in_specs=[
            pl.BlockSpec((sources, 1, slots, GROUP, share), lambda i, j: (0, i, 0, j, 0)),
            pl.BlockSpec((cols, 1), lambda i, j: (0, 0)),
            pl.BlockSpec((1, cols, rank), lambda i, j: (0, j, 0)),
        ],
        out_specs=(
            pl.BlockSpec((share, cols), lambda i, j: (i, j)),
            pl.BlockSpec((share, rank), lambda i, j: (i, 0)),
        ),
        scratch_shapes=[
            pltpu.VMEM((cols, cols), jnp.bfloat16),
            pltpu.VMEM((share, rank), jnp.float32),
        ],
        compiler_params=pltpu.CompilerParams(vmem_limit_bytes=40 * 2**20),
        name="place",
    )(received, column, cross_down)


PIECES = 4


def reduce_kernel(groups, term_ref, low_ref, near_in, held, far_in, *sems):
    b, m = lax.axis_index("batch"), lax.axis_index("mp")
    near_send, near_recv, far_send, far_recv, back_send, back_recv = sems
    near = (b, partner(m, 1, groups))
    far = [(b, partner(m, 1 << (s + 1), groups)) for s in range(far_in.shape[0])]
    half = term_ref.shape[0] // 2
    piece = half // PIECES
    core = m % 2

    def rows(who, k):
        return pl.ds(pl.multiple_of(who * half + k * piece, piece), piece)

    barrier = pltpu.get_barrier_semaphore()
    for peer in [near] + far:
        pl.semaphore_signal(barrier, inc=1, device_id=peer, device_id_type=MESH)
    pl.semaphore_wait(barrier, 1 + len(far))

    def send(src, dst, send_sem, recv_sem, peer):
        copy = pltpu.make_async_remote_copy(
            src_ref=src,
            dst_ref=dst,
            send_sem=send_sem,
            recv_sem=recv_sem,
            device_id=peer,
            device_id_type=MESH,
        )
        copy.start()
        return copy

    sent = []
    going = [
        send(term_ref.at[rows(1 - core, k)], near_in.at[k], near_send.at[k], near_recv.at[k], near)
        for k in range(PIECES)
    ]
    for s in range(len(far) + 1):
        arriving, going = going, []
        for k in range(PIECES):
            arriving[k].wait_recv()
            if s == 0:
                mine, other = term_ref[rows(core, k)], near_in[k]
            else:
                mine, other = held[s - 1, k], far_in[s - 1, k]
            total = (mine.astype(jnp.float32) + other.astype(jnp.float32)).astype(jnp.bfloat16)
            if s < len(far):
                held[s, k] = total
                going.append(
                    send(
                        held.at[s, k], far_in.at[s, k], far_send.at[s, k], far_recv.at[s, k], far[s]
                    )
                )
            else:
                place = rows(core, k)
                low_ref[place] = total
                going.append(
                    send(low_ref.at[place], low_ref.at[place], back_send.at[k], back_recv.at[k], near)
                )
        sent += arriving
    for copy in going:
        copy.wait_recv()
    for copy in sent + going:
        copy.wait_send()


def reduce_over_mp(term):
    groups = lax.axis_size("mp")
    stages = groups.bit_length() - 2
    rows, rank = term.shape
    block = (PIECES, rows // 2 // PIECES, rank)
    dma = pltpu.SemaphoreType.DMA
    return pl.pallas_call(
        functools.partial(reduce_kernel, groups),
        out_shape=jax.ShapeDtypeStruct(term.shape, term.dtype),
        in_specs=[pl.BlockSpec(memory_space=pltpu.VMEM)],
        out_specs=pl.BlockSpec(memory_space=pltpu.VMEM),
        scratch_shapes=[
            pltpu.VMEM(block, term.dtype),
            pltpu.VMEM((stages,) + block, term.dtype),
            pltpu.VMEM((stages,) + block, term.dtype),
            dma((PIECES,)),
            dma((PIECES,)),
            dma((stages, PIECES)),
            dma((stages, PIECES)),
            dma((PIECES,)),
            dma((PIECES,)),
        ],
        compiler_params=pltpu.CompilerParams(
            collective_id=1, has_side_effects=True, vmem_limit_bytes=24 * 2**20
        ),
        name="reduce",
    )(term)


def per_device(lookup_ids, table_feature, tables, cross_down, cross_up, cross_bias):
    slots_local = tables.shape[0]
    feats = table_feature.shape[0]
    sources = lax.axis_size("batch")
    groups = lax.axis_size("mp")
    examples_local = lookup_ids.shape[1] // sources
    share = examples_local // groups
    start = lax.axis_index("mp") * share
    by_owner = lookup_ids.reshape(slots_local, sources, examples_local)
    wanted = lax.dynamic_slice_in_dim(by_owner, start, share, 2)
    wanted = wanted.reshape(slots_local * sources * share)
    received = exchange(gather(wanted, tables, sources, groups, share))
    column = (table_feature[:, None] + feats * jnp.arange(GROUP)[None, :]).reshape(-1, 1)
    embedded, term = place(received, column, cross_down)
    embedded_wide = embedded.astype(jnp.float32)
    state = embedded
    for layer in range(len(cross_down)):
        if layer > 0:
            term = jnp.dot(state, cross_down[layer], preferred_element_type=jnp.float32)
            term = term.astype(jnp.bfloat16)
        low = reduce_over_mp(term)
        high = (
            jnp.dot(low, cross_up[layer], preferred_element_type=jnp.float32)
            + cross_bias[layer][None, :]
        )
        state = (embedded_wide * high + state.astype(jnp.float32)).astype(jnp.bfloat16)
    return state


def solution(mesh):
    return jax.shard_map(
        per_device,
        mesh=mesh,
        in_specs=(
            P("batch", None),
            P(),
            P("batch", None, None),
            P(None, "mp", None),
            P(None, None, "mp"),
            P(None, "mp"),
        ),
        out_specs=P("batch", "mp"),
        check_vma=False,
    )
```

profile of v0, /device:TPU:0, one launch (start us, length us, event | category | flops | bytes accessed | tf_op | source)
XLA Modules:
  0.0 362.8 jit_solution(10604554340199990801)
XLA Ops:
  0.0 0.0 copy-start
  0.0 1.0 copy-done
  1.0 0.8 fusion.9
  1.9 0.7 broadcast_add_fusion
  2.6 0.1 copy.12
  2.7 0.3 add.65.column_ref
  3.0 46.0 %lookup.1.src_ref = bf16[8,4,8,32,512]{4,3,2,1,0:T(8,128)(2,1)S(1)} custom-call(s32[32768]{0:T(1024)S(1)} %bitcast.20, bf16[8,8192,128]{2,1,0:T(8,128)(2,1)} %table_ref.1), custom_call_target="tpu_custom_call" | custom-call | tf_op jit(solution)/shard_map/lookup/pallas_call | solution.py:45
  49.0 0.0 copy-start.2
  49.0 3.4 copy-done.2
  52.4 203.8 %exchange.1.x_ref = bf16[8,4,8,32,512]{4,3,2,1,0:T(8,128)(2,1)} custom-call(bf16[8,4,8,32,512]{4,3,2,1,0:T(8,128)(2,1)} %copy-done.2), custom_call_target="tpu_custom_call" | custom-call | tf_op jit(solution)/shard_map/exchange/pallas_call | solution.py:110
  256.3 0.0 copy-start.3
  256.3 2.2 copy-done.3
  258.5 0.0 copy-start.5
  258.5 18.4 %place.1 = (bf16[2048,2048]{1,0:T(8,128)(2,1)}, bf16[2048,512]{1,0:T(8,128)(2,1)S(1)}) custom-call(bf16[8,4,8,32,512]{4,3,2,1,0:T(8,128)(2,1)} %exchange.1.x_ref, s32[1024,1]{1,0:T(8,128)S(1)} %add.65.column_ref, bf16[2,2048,512]{2,1,0:T(8,128)(2,1)S(1)} %copy-done.3), custom_call_target="tpu_custom_call" | custom-call | tf_op jit(solution)/shard_map/place/pallas_call | solution.py:158
  276.9 28.0 %reduce.2 = bf16[2048,512]{1,0:T(8,128)(2,1)S(1)} custom-call(bf16[2048,512]{1,0:T(8,128)(2,1)S(1)} %get-tuple-element.8.term_ref), custom_call_target="tpu_custom_call" | custom-call | tf_op jit(solution)/shard_map/reduce/pallas_call | solution.py:255
  304.9 0.0 copy-done.5
  304.9 0.0 copy-start.4
  304.9 10.1 %fusion.2 = bf16[2048,2048]{1,0:T(8,128)(2,1)} fusion(bf16[2048,2048]{1,0:T(8,128)(2,1)} %get-tuple-element.7, f32[2048]{0:T(1024)S(1)} %bitcast.23, bf16[2048,512]{1,0:T(8,128)(2,1)S(1)} %reduce.2, bf16[2,512,2048]{2,1,0:T(8,128)(2,1)S(1)} %copy-done.5), kind=kOutput, calls=%fused_computation.4 | convolution fusion | flops 4315938816 | bytes 20979712 | tf_op jit(solution)/shard_map/dot_general | solution.py:300
  315.0 0.0 copy-done.4
  315.0 8.1 %convolution_convert_fusion.term_ref = bf16[2048,512]{1,0:T(8,128)(2,1)S(1)} fusion(bf16[2048,2048]{1,0:T(8,128)(2,1)} %fusion.2, bf16[2,2048,512]{2,1,0:T(8,128)(2,1)S(1)} %copy-done.4), kind=kOutput, calls=%fused_computation.5 | convolution fusion | flops 4296015872 | bytes 12582912 | tf_op jit(solution)/shard_map/dot_general | solution.py:296
  323.1 28.4 %reduce.3 = bf16[2048,512]{1,0:T(8,128)(2,1)S(1)} custom-call(bf16[2048,512]{1,0:T(8,128)(2,1)S(1)} %convolution_convert_fusion.term_ref), custom_call_target="tpu_custom_call" | custom-call | tf_op jit(solution)/shard_map/reduce/pallas_call | solution.py:255
  351.5 0.0 copy-start.1
  351.5 11.3 %fusion.1 = bf16[2048,2048]{1,0:T(8,128)(2,1)} fusion(bf16[2048,2048]{1,0:T(8,128)(2,1)} %get-tuple-element.7, bf16[2048,2048]{1,0:T(8,128)(2,1)} %fusion.2, f32[2048]{0:T(1024)S(1)} %bitcast.22, bf16[2048,512]{1,0:T(8,128)(2,1)S(1)} %reduce.3, bf16[2,512,2048]{2,1,0:T(8,128)(2,1)S(1)} %copy-done.5), kind=kOutput, calls=%fused_computation.3 | convolution fusion | flops 4320133120 | bytes 29368320 | tf_op jit(solution)/shard_map/dot_general | solution.py:300
  362.8 0.0 copy-done.1
  (3 shorter events, 0.0 us)
Async XLA Ops:
  0.0 1.0 copy-start
  49.0 3.4 copy-start.2
  256.3 2.2 copy-start.3
  258.5 46.4 %copy-start.5 = (bf16[2,512,2048]{2,1,0:T(8,128)(2,1)S(1)}, bf16[2,512,2048]{2,1,0:T(8,128)(2,1)}, u32[]{:S(2)}) copy-start(bf16[2,512,2048]{2,1,0:T(8,128)(2,1)} %param.10) | copy-start | bytes 12582916
  304.9 10.1 %copy-start.4 = (bf16[2,2048,512]{2,1,0:T(8,128)(2,1)S(1)}, bf16[2,2048,512]{2,1,0:T(8,128)(2,1)}, u32[]{:S(2)}) copy-start(bf16[2,2048,512]{2,1,0:T(8,128)(2,1)} %down_ref.1) | copy-start | bytes 12582916
  351.5 11.3 %copy-start.1 = (s32[8,16384]{1,0:T(8,128)S(1)}, s32[8,16384]{1,0:T(8,128)}, u32[]{:S(2)}) copy-start(s32[8,16384]{1,0:T(8,128)} %param.6) | copy-start | bytes 1572868
where the time goes:
time: 363 us
  Pallas kernels  325 us (90%)
  matrix products  29.4 us (8%)
  local copies, waits for them, and re-layouts  7.86 us (2%)
    pallas_call x1, Pallas kernels, exchange(): pl.pallas_call(functools.partial(exchange_kernel, sources, groups), out_s...  204 us
    pallas_call x2, Pallas kernels, reduce_over_mp(): pl.pallas_call(functools.partial(reduce_kernel, groups), out_shape=jax.Sh...  56.4 us
    pallas_call x1, Pallas kernels, gather(): pl.pallas_call(gather_kernel, out_shape=jax.ShapeDtypeStruct((sources, gr...  46 us
    dot_general x2, matrix products, per_device(): jnp.dot(low, cross_up[layer], preferred_element_type=jnp.float32)  21.3 us
    pallas_call x1, Pallas kernels, place(): pl.pallas_call(place_kernel, out_shape=(jax.ShapeDtypeStruct((groups * sh...  18.4 us
    dot_general x1, matrix products, per_device(): term = jnp.dot(state, cross_down[layer], preferred_element_type=jnp.float32)  8.11 us

commit v1 on v0

v1 whole, which is shorter than its diff:
```python
import functools

import jax
import jax.numpy as jnp
from jax import lax
from jax.experimental import pallas as pl
from jax.experimental.pallas import tpu as pltpu
from jax.sharding import PartitionSpec as P

MESH = pl.DeviceIdType.MESH
GROUP = 16
LANES = 128
CORES = 2
UNROLL = 32
TILES = 4


def partner(me, mask, size):
    other = me
    bit = 1
    while bit < size:
        if mask & bit:
            other = other + bit * (1 - 2 * ((me // bit) % 2))
        bit *= 2
    return other


def kernel(
    sources,
    groups,
    feature_ref,
    bias_ref,
    ids_ref,
    tables_ref,
    down_ref,
    up_ref,
    out_ref,
    ids,
    stage,
    wide,
    rows,
    sent,
    received,
    down,
    up,
    placing,
    emb,
    mid,
    result,
    term,
    near_in,
    held,
    far_in,
    low,
    ids_sem,
    stage_sem,
    weight_sem,
    send_sem,
    recv_sem,
    reduce_send,
    reduce_recv,
    out_sem,
):
    b, m = lax.axis_index("batch"), lax.axis_index("mp")
    core = m % CORES
    side = m // CORES
    chunks, blocks, slots, emb_local, part = sent.shape
    pairs = slots // 2
    buckets = tables_ref.shape[1]
    emb_dim = tables_ref.shape[2]
    shared = emb_dim // 2
    width = down.shape[1]
    cols = placing.shape[0]
    feats = feature_ref.shape[0]
    near = (b, partner(m, 1, groups))
    far = (b, partner(m, CORES, groups))
    peers = [
        (partner(b, x, sources), side * CORES + partner(core, y, CORES), partner(core, y, CORES))
        for x in range(sources - 1, -1, -1)
        for y in range(CORES - 1, -1, -1)
        if (x, y) != (0, 0)
    ]

    ids_copy = pltpu.make_async_copy(ids_ref, ids, ids_sem)
    ids_copy.start()
    half = buckets // 2

    def stage_copies(p, h):
        span = pl.ds(h * half, half)
        return [
            pltpu.make_async_copy(
                tables_ref.at[2 * p + side, span], stage.at[h, 0], stage_sem.at[h, 0]
            ),
            pltpu.make_async_copy(
                tables_ref.at[2 * p + 1 - side, span], stage.at[h, 1], stage_sem.at[h, 1]
            ),
        ]

    for h in range(2):
        for copy in stage_copies(0, h):
            copy.start()
    weights = [
        pltpu.make_async_copy(down_ref, down, weight_sem.at[0]),
        pltpu.make_async_copy(up_ref, up, weight_sem.at[1]),
    ]

    barrier = pltpu.get_barrier_semaphore()
    greeted = [(x, y) for x, y, _ in peers] + [far]
    for peer in greeted:
        pl.semaphore_signal(barrier, inc=1, device_id=peer, device_id_type=MESH)

    def convert(p):
        for h in range(2):
            for copy in stage_copies(p, h):
                copy.wait()
            step = min(256, half)

            @pl.loop(0, half // step)
            def _(i):
                at = pl.ds(pl.multiple_of(i * step, step), step)
                to = pl.ds(pl.multiple_of(p * buckets + h * half + i * step, step), step)
                lane = lax.broadcasted_iota(jnp.int32, (step, emb_dim), 1)
                own = stage[h, 0, at, :].astype(jnp.float32)
                other = pltpu.roll(stage[h, 1, at, :].astype(jnp.float32), shared, 1)
                wide[to, :] = jnp.where(lane // shared == side, own, other)

            @pl.when(p + 1 < pairs)
            def _():
                for copy in stage_copies(p + 1, h):
                    copy.start()

    def gather(k, p):
        count = sources * part
        first = (k * pairs + p) * 2 * count
        lower = lax.broadcasted_iota(jnp.int32, (1, emb_dim), 1) < shared

        @pl.loop(0, count // UNROLL)
        def _(i):
            base = pl.multiple_of(i * UNROLL, UNROLL)
            for u in range(UNROLL):
                a = ids[first + base + u]
                c = ids[first + count + base + u]
                rows[pl.ds(base + u, 1), :] = jnp.where(
                    lower, wide[pl.ds(a, 1), :], wide[pl.ds(c, 1), :]
                )

        for d in range(sources):
            turned = rows[d * part : (d + 1) * part, :].T.astype(jnp.bfloat16)
            for s in range(2):
                for c in range(CORES):
                    at = s * shared + c * emb_local
                    sent[k, d * CORES + c, 2 * p + s] = turned[at : at + emb_local]

    def send(k):
        for x, y, c in peers:
            pltpu.make_async_remote_copy(
                src_ref=sent.at[k, x * CORES + c],
                dst_ref=received.at[k, core * sources + b],
                send_sem=send_sem.at[k],
                recv_sem=recv_sem.at[k],
                device_id=(x, y),
                device_id_type=MESH,
            ).start()
        received[k, core * sources + b] = sent[k, b * CORES + core]

    def exchanged(k):
        span = pl.ds(0, blocks - 1)
        return pltpu.make_async_remote_copy(
            src_ref=sent.at[k, span],
            dst_ref=received.at[k, span],
            send_sem=send_sem.at[k],
            recv_sem=recv_sem.at[k],
            device_id=near,
            device_id_type=MESH,
        )

    ids_copy.wait()

    @pl.loop(0, pairs)
    def _(p):
        convert(p)
        gather(0, p)

    pl.semaphore_wait(barrier, len(greeted))
    send(0)
    for copy in weights:
        copy.start()

    @pl.loop(1, chunks)
    def _(k):
        @pl.loop(0, pairs)
        def _(p):
            gather(k, p)

        send(k)

    @pl.loop(0, feats)
    def _(s):
        column = lax.broadcasted_iota(jnp.int32, (GROUP, cols), 1)
        e = lax.broadcasted_iota(jnp.int32, (GROUP, cols), 0)
        placing[pl.ds(pl.multiple_of(s * GROUP, GROUP), GROUP), :] = jnp.where(
            column == feature_ref[s] + feats * e, 1.0, 0.0
        ).astype(jnp.bfloat16)

    for copy in weights:
        copy.wait()

    size = 2 * part
    mine = pl.ds(pl.multiple_of(core * part, part), part)
    theirs = pl.ds(pl.multiple_of((1 - core) * part, part), part)

    def remote(src, dst, kind, layer, slot, peer):
        return pltpu.make_async_remote_copy(
            src_ref=src,
            dst_ref=dst,
            send_sem=reduce_send.at[kind, layer, slot],
            recv_sem=reduce_recv.at[kind, layer, slot],
            device_id=peer,
            device_id_type=MESH,
        )

    def to_near(layer, slot):
        return remote(
            term.at[layer, slot, theirs], near_in.at[layer, slot], 0, layer, slot, near
        )

    def to_far(layer, slot):
        return remote(held.at[layer, slot], far_in.at[layer, slot], 1, layer, slot, far)

    def back(layer, slot):
        place = low.at[layer, slot, mine]
        return remote(place, place, 2, layer, slot, near)

    def reduce_middle(layer, slot):
        to_near(layer, slot).wait_recv()
        held[layer, slot] = (
            term[layer, slot, mine].astype(jnp.float32) + near_in[layer, slot].astype(jnp.float32)
        ).astype(jnp.bfloat16)
        to_far(layer, slot).start()

    def reduce_last(layer, slot):
        to_far(layer, slot).wait_recv()
        low[layer, slot, mine] = (
            held[layer, slot].astype(jnp.float32) + far_in[layer, slot].astype(jnp.float32)
        ).astype(jnp.bfloat16)
        back(layer, slot).start()

    def reduce_done(layer, slot):
        back(layer, slot).wait_recv()
        to_near(layer, slot).wait_send()
        to_far(layer, slot).wait_send()
        back(layer, slot).wait_send()

    def enter(k, slot):
        exchanged(k).wait_recv()
        for j in range(emb_local // GROUP):
            sides = [
                received[
                    k, h * sources : (h + 1) * sources, :, j * GROUP : (j + 1) * GROUP
                ].reshape(cols, part)
                for h in range(2)
            ]
            emb[slot, :, j * cols : (j + 1) * cols] = lax.dot_general(
                jnp.concatenate(sides, axis=1),
                placing[...],
                (((0,), (0,)), ((), ())),
                preferred_element_type=jnp.float32,
            ).astype(jnp.bfloat16)
        term[0, slot] = jnp.dot(
            emb[slot], down[0], preferred_element_type=jnp.float32
        ).astype(jnp.bfloat16)
        to_near(0, slot).start()

    tile = width // TILES

    def cross(layer, slot, state, new):
        for n in range(TILES):
            at = slice(n * tile, (n + 1) * tile)
            high = (
                jnp.dot(low[layer, slot], up[layer, :, at], preferred_element_type=jnp.float32)
                + bias_ref[layer, at][None, :]
            )
            new[slot, :, at] = (
                emb[slot, :, at].astype(jnp.float32) * high
                + state[slot, :, at].astype(jnp.float32)
            ).astype(jnp.bfloat16)

    def out_copies(k, slot):
        return [
            pltpu.make_async_copy(
                result.at[slot, pl.ds(h * part, part)],
                out_ref.at[pl.ds(pl.multiple_of((h * chunks + k) * part, part), part)],
                out_sem.at[slot, h],
            )
            for h in range(2)
        ]

    @pl.loop(0, chunks + 1)
    def _(k):
        slot = k % 2
        last = (k + 1) % 2

        @pl.when(k < chunks)
        def _():
            enter(k, slot)

        @pl.when(k > 0)
        def _():
            reduce_middle(1, last)

        @pl.when(k < chunks)
        def _():
            reduce_middle(0, slot)

        @pl.when(k > 0)
        def _():
            reduce_last(1, last)

        @pl.when(k < chunks)
        def _():
            reduce_last(0, slot)

        @pl.when(k > 0)
        def _():
            reduce_done(1, last)

            @pl.when(k > 2)
            def _():
                for copy in out_copies(k - 3, last):
                    copy.wait()

            cross(1, last, mid, result)
            for copy in out_copies(k - 1, last):
                copy.start()

        @pl.when(k < chunks)
        def _():
            reduce_done(0, slot)
            cross(0, slot, emb, mid)
            term[1, slot] = jnp.dot(
                mid[slot], down[1], preferred_element_type=jnp.float32
            ).astype(jnp.bfloat16)
            to_near(1, slot).start()

    for k in range(max(chunks - 2, 0), chunks):
        for copy in out_copies(k, k % 2):
            copy.wait()

    @pl.loop(0, chunks)
    def _(k):
        exchanged(k).wait_send()


def pipeline(table_feature, bias, ids, tables, cross_down, cross_up, chunks, sources, groups):
    slots, buckets, emb_dim = tables.shape
    layers, width, rank = cross_down.shape
    feats = table_feature.shape[0]
    emb_local = emb_dim // groups
    part = LANES
    size = 2 * part
    pairs = slots // 2
    blocks = CORES * sources
    dma = pltpu.SemaphoreType.DMA
    bf16, f32 = jnp.bfloat16, jnp.float32
    return pl.pallas_call(
        functools.partial(kernel, sources, groups),
        out_shape=jax.ShapeDtypeStruct((chunks * size, width), bf16),
        in_specs=[
            pl.BlockSpec(memory_space=pltpu.SMEM),
            pl.BlockSpec(memory_space=pltpu.VMEM),
        ]
        + [pl.BlockSpec(memory_space=pl.ANY)] * 4,
        out_specs=pl.BlockSpec(memory_space=pl.ANY),
        scratch_shapes=[
            pltpu.SMEM(ids.shape, jnp.int32),
            pltpu.VMEM((2, 2, buckets // 2, emb_dim), bf16),
            pltpu.VMEM((pairs * buckets, emb_dim), f32),
            pltpu.VMEM((sources * part, emb_dim), f32),
            pltpu.VMEM((chunks, blocks, slots, emb_local, part), bf16),
            pltpu.VMEM((chunks, blocks, slots, emb_local, part), bf16),
            pltpu.VMEM((layers, width, rank), bf16),
            pltpu.VMEM((layers, rank, width), bf16),
            pltpu.VMEM((feats * GROUP, feats * GROUP), bf16),
            pltpu.VMEM((2, size, width), bf16),
            pltpu.VMEM((2, size, width), bf16),
            pltpu.VMEM((2, size, width), bf16),
            pltpu.VMEM((layers, 2, size, rank), bf16),
            pltpu.VMEM((layers, 2, part, rank), bf16),
            pltpu.VMEM((layers, 2, part, rank), bf16),
            pltpu.VMEM((layers, 2, part, rank), bf16),
            pltpu.VMEM((layers, 2, size, rank), bf16),
            dma,
            dma((2, 2)),
            dma((2,)),
            dma((chunks,)),
            dma((chunks,)),
            dma((3, layers, 2)),
            dma((3, layers, 2)),
            dma((2, 2)),
        ],
        compiler_params=pltpu.CompilerParams(
            collective_id=0, has_side_effects=True, vmem_limit_bytes=67_043_328
        ),
        name="pipeline",
    )(table_feature, bias, ids, tables, cross_down, cross_up)


def per_device(lookup_ids, table_feature, tables, cross_down, cross_up, cross_bias):
    slots, buckets, _ = tables.shape
    sources = lax.axis_size("batch")
    groups = lax.axis_size("mp")
    examples = lookup_ids.shape[1] // sources
    mine = examples // CORES
    chunks = mine // LANES
    start = (lax.axis_index("mp") % CORES) * mine
    wanted = lax.dynamic_slice_in_dim(
        lookup_ids.reshape(slots, sources, examples), start, mine, 2
    ).reshape(slots // 2, 2, sources, chunks, LANES)
    wanted = wanted + buckets * jnp.arange(slots // 2, dtype=jnp.int32)[:, None, None, None, None]
    ids = wanted.transpose(3, 0, 1, 2, 4).reshape(-1)
    return pipeline(
        table_feature, cross_bias, ids, tables, cross_down, cross_up, chunks, sources, groups
    )


def solution(mesh):
    return jax.shard_map(
        per_device,
        mesh=mesh,
        in_specs=(
            P("batch", None),
            P(),
            P("batch", None, None),
            P(None, "mp", None),
            P(None, None, "mp"),
            P(None, "mp"),
        ),
        out_specs=P("batch", "mp"),
        check_vma=False,
    )
```

time: 363 us -> 244 us (0.67)
  Pallas kernels: 325 us -> 234 us
  matrix products: 29.4 us -> 0 us
    pallas_call x5 -> x1, Pallas kernels: 325 us -> 234 us  [pipeline(): pl.pallas_call(functools.partial(kernel, sources, groups), out_shape=jax....]
    dot_general x3 -> x0, matrix products: 29.4 us -> none  [the longest x2 21.3 us: per_device(): jnp.dot(low, cross_up[layer], preferred_element_type=jnp.float32)]
    unnamed x14 -> x3, local copies, waits for them, and re-layouts: 6.75 us -> 9.46 us
where the time goes in v1:
time: 244 us
  Pallas kernels  234 us (96%)
  local copies, waits for them, and re-layouts  10.2 us (4%)
    pallas_call x1, Pallas kernels, pipeline(): pl.pallas_call(functools.partial(kernel, sources, groups), out_shape=jax....  234 us
    unnamed x3, local copies, waits for them, and re-layouts  9.46 us

profile of v1, /device:TPU:0, one launch (start us, length us, event | category | flops | bytes accessed | tf_op | source)
XLA Modules:
  0.0 244.1 jit_solution(9134265512644335748)
XLA Ops:
  0.0 1.0 dynamic-slice_bitcast_fusion
  1.0 0.1 fusion
  1.1 0.8 copy.8
  1.9 233.8 %pipeline.1 = bf16[2048,2048]{1,0:T(8,128)(2,1)} custom-call(s32[64]{0:T(128)} %feature_ref.1, f32[2,2048]{1,0:T(2,128)} %bias_ref.1, s32[65536]{0:T(1024)} %bitcast.11, bf16[8,8192,128]{2,1,0:T(8,128)(2,1)} %tables_ref.1, bf16[2,2048,512]{2,1,0:T(8,128)(2,1)} %down_ref.1, bf16[2,512,2048]{2,1,0:T(8,128)(2,1)} %up_ref.1), custom_call_target="tpu_custom_call" | custom-call | tf_op jit(solution)/shard_map/pipeline/pallas_call | solution.py:365
  235.7 8.4 %copy.16 = bf16[2048,2048]{1,0:T(8,128)(2,1)} copy(bf16[2048,2048]{1,0:T(8,128)(2,1)} %pipeline.1) | data formatting | bytes 16777216
  (2 shorter events, 0.1 us)

commit v2 on v1

v2 whole, which is shorter than its diff:
```python
import functools

import jax
import jax.numpy as jnp
from jax import lax
from jax.experimental import pallas as pl
from jax.experimental.pallas import tpu as pltpu
from jax.sharding import PartitionSpec as P

MESH = pl.DeviceIdType.MESH
GROUP = 16
LANES = 128
CORES = 2
TILES = 4
AHEAD = 3
PHASES = 4
STEPS = 4
PIECES = 16
LIMIT = 67_043_328


def partner(me, mask, size):
    other = me
    bit = 1
    while bit < size:
        if mask & bit:
            other = other + bit * (1 - 2 * ((me // bit) % 2))
        bit *= 2
    return other


def kernel(
    sources,
    groups,
    feature_ref,
    bias_ref,
    ids_ref,
    tables_ref,
    down_ref,
    up_ref,
    out_ref,
    ids,
    stage,
    wide,
    rows,
    sent,
    received,
    down,
    up,
    placing,
    emb,
    mid,
    result,
    term,
    near_in,
    held,
    far_in,
    low,
    ids_sem,
    stage_sem,
    weight_sem,
    send_sem,
    recv_sem,
    reduce_send,
    reduce_recv,
    out_sem,
):
    b, m = lax.axis_index("batch"), lax.axis_index("mp")
    core = m % CORES
    side = m // CORES
    chunks, blocks, slots, emb_local, part = received.shape
    ring = sent.shape[0]
    pairs = slots // 2
    buckets = tables_ref.shape[1]
    emb_dim = tables_ref.shape[2]
    shared = emb_dim // 2
    width = down.shape[1]
    cols = placing.shape[0]
    feats = feature_ref.shape[0]
    near = (b, partner(m, 1, groups))
    far = (b, partner(m, CORES, groups))
    peers = [
        (partner(b, x, sources), side * CORES + partner(core, y, CORES), partner(core, y, CORES))
        for x in range(sources - 1, -1, -1)
        for y in range(CORES - 1, -1, -1)
        if (x, y) != (0, 0)
    ]

    def ids_copy(k, d):
        start = d * (2 * chunks * part) + (core * chunks + k) * part
        return pltpu.make_async_copy(
            ids_ref.at[:, pl.ds(pl.multiple_of(start, part), part)], ids.at[k, d], ids_sem.at[k]
        )

    span = buckets // STEPS

    def stage_copy(i):
        return pltpu.make_async_copy(
            tables_ref.at[pl.ds(2 * (i // STEPS), 2), pl.ds(i % STEPS * span, span)],
            stage.at[i % 2],
            stage_sem.at[i % 2],
        )

    stage_copy(0).start()
    for d in range(sources):
        ids_copy(0, d).start()
    stage_copy(1).start()

    barrier = pltpu.get_barrier_semaphore()
    greeted = [(x, y) for x, y, _ in peers] + [far]
    for peer in greeted:
        pl.semaphore_signal(barrier, inc=1, device_id=peer, device_id_type=MESH)

    @pl.loop(1, chunks)
    def _(k):
        for d in range(sources):
            ids_copy(k, d).start()

    weights = [
        pltpu.make_async_copy(down_ref, down, weight_sem.at[0]),
        pltpu.make_async_copy(up_ref, up, weight_sem.at[1]),
    ]

    def convert(p):
        for i in range(p * STEPS, (p + 1) * STEPS):
            stage_copy(i).wait()
            step = min(1024, span)

            @pl.loop(0, span // step)
            def _(t, i=i):
                at = pl.ds(pl.multiple_of(t * step, step), step)
                to = pl.ds(pl.multiple_of(i * span + t * step, step), step)
                lane = lax.broadcasted_iota(jnp.int32, (step, emb_dim), 1)
                own = stage[i % 2, side, at, :].astype(jnp.float32)
                other = pltpu.roll(stage[i % 2, 1 - side, at, :].astype(jnp.float32), shared, 1)
                wide[to, :] = jnp.where(lane // shared == side, own, other)

            if i + 2 < pairs * STEPS:
                stage_copy(i + 2).start()

    def gather(k, p):
        lower = lax.broadcasted_iota(jnp.int32, (1, emb_dim), 1) < shared
        table = wide.at[pl.ds(p * buckets, buckets)]

        @pl.loop(0, sources)
        def _(d):
            base = pl.multiple_of(d * part, part)
            for u in range(part):
                one = table[pl.ds(ids[k, d, 2 * p, u], 1), :]
                two = table[pl.ds(ids[k, d, 2 * p + 1, u], 1), :]
                rows[pl.ds(base + u, 1), :] = jnp.where(lower, one, two)

        for d in range(sources):
            turned = rows[d * part : (d + 1) * part, :].T.astype(jnp.bfloat16)
            for s in range(2):
                for c in range(CORES):
                    at = s * shared + c * emb_local
                    sent[k % ring, d * CORES + c, 2 * p + s] = turned[at : at + emb_local]

    def send(k, span):
        for x, y, c in peers:
            pltpu.make_async_remote_copy(
                src_ref=sent.at[k % ring, x * CORES + c, span],
                dst_ref=received.at[k, core * sources + b, span],
                send_sem=send_sem.at[k],
                recv_sem=recv_sem.at[k],
                device_id=(x, y),
                device_id_type=MESH,
            ).start()

    def keep(k):
        received[k, core * sources + b] = sent[k % ring, b * CORES + core]

    def exchanged(k):
        span = pl.ds(0, blocks - 1)
        return pltpu.make_async_remote_copy(
            src_ref=sent.at[k % ring, span],
            dst_ref=received.at[k, span],
            send_sem=send_sem.at[k],
            recv_sem=recv_sem.at[k],
            device_id=near,
            device_id_type=MESH,
        )

    def ids_wait(k):
        pltpu.make_async_copy(ids.at[k], ids.at[k], ids_sem.at[k]).wait()

    ids_wait(0)
    for p in range(pairs):
        convert(p)
        gather(0, p)
        if p == 0:
            pl.semaphore_wait(barrier, len(greeted))
        send(0, pl.ds(2 * p, 2))
    keep(0)
    for copy in weights:
        copy.start()

    @pl.loop(1, min(AHEAD, chunks))
    def _(k):
        ids_wait(k)
        for p in range(pairs):
            gather(k, p)
        send(k, pl.ds(0, slots))
        keep(k)

    @pl.loop(0, feats)
    def _(s):
        column = lax.broadcasted_iota(jnp.int32, (GROUP, cols), 1)
        e = lax.broadcasted_iota(jnp.int32, (GROUP, cols), 0)
        placing[pl.ds(pl.multiple_of(s * GROUP, GROUP), GROUP), :] = jnp.where(
            column == feature_ref[s] + feats * e, 1.0, 0.0
        ).astype(jnp.bfloat16)

    for copy in weights:
        copy.wait()

    share = part // 2
    mine = pl.ds(pl.multiple_of(core * share, share), share)
    theirs = pl.ds(pl.multiple_of((1 - core) * share, share), share)

    def remote(src, dst, kind, layer, h, peer):
        return pltpu.make_async_remote_copy(
            src_ref=src,
            dst_ref=dst,
            send_sem=reduce_send.at[kind, layer, h],
            recv_sem=reduce_recv.at[kind, layer, h],
            device_id=peer,
            device_id_type=MESH,
        )

    def to_near(layer, h):
        return remote(term.at[layer, h, theirs], near_in.at[layer, h], 0, layer, h, near)

    def to_far(layer, h):
        return remote(held.at[layer, h], far_in.at[layer, h], 1, layer, h, far)

    def back(layer, h):
        place = low.at[layer, h, mine]
        return remote(place, place, 2, layer, h, near)

    def reduce_middle(layer, h):
        to_near(layer, h).wait_recv()
        held[layer, h] = (
            term[layer, h, mine].astype(jnp.float32) + near_in[layer, h].astype(jnp.float32)
        ).astype(jnp.bfloat16)
        to_far(layer, h).start()

    def reduce_last(layer, h):
        to_far(layer, h).wait_recv()
        low[layer, h, mine] = (
            held[layer, h].astype(jnp.float32) + far_in[layer, h].astype(jnp.float32)
        ).astype(jnp.bfloat16)
        back(layer, h).start()

    def reduce_done(layer, h):
        back(layer, h).wait_recv()
        to_near(layer, h).wait_send()
        to_far(layer, h).wait_send()
        back(layer, h).wait_send()

    def project(layer, h, state):
        term[layer, h] = jnp.dot(
            state[h], down[layer], preferred_element_type=jnp.float32
        ).astype(jnp.bfloat16)
        to_near(layer, h).start()

    def enter(k, h):
        for j in range(emb_local // GROUP):
            x = received[k, h * sources : (h + 1) * sources, :, j * GROUP : (j + 1) * GROUP]
            emb[h, :, j * cols : (j + 1) * cols] = lax.dot_general(
                x.reshape(cols, part),
                placing[...],
                (((0,), (0,)), ((), ())),
                preferred_element_type=jnp.float32,
            ).astype(jnp.bfloat16)
        project(0, h, emb)

    tile = width // TILES

    def cross(layer, h, state, store):
        for n in range(TILES):
            at = slice(n * tile, (n + 1) * tile)
            high = (
                jnp.dot(low[layer, h], up[layer, :, at], preferred_element_type=jnp.float32)
                + bias_ref[layer, at][None, :]
            )
            store(
                at,
                (
                    emb[h, :, at].astype(jnp.float32) * high + state[h, :, at].astype(jnp.float32)
                ).astype(jnp.bfloat16),
            )

    def out_copy(k, h):
        span = pl.ds(pl.multiple_of((h * chunks + k) * part, part), part)
        return pltpu.make_async_copy(result.at[h], out_ref.at[span], out_sem.at[h])

    @pl.loop(0, chunks)
    def _(k):
        ahead = k + AHEAD
        more = ahead < chunks

        def look_up(phase):
            for p in range(pairs):
                if p * PHASES // pairs == phase:

                    @pl.when(more)
                    def _(p=p):
                        gather(ahead, p)

        @pl.when(more)
        def _():
            ids_wait(ahead)

            @pl.when(ahead >= ring)
            def _():
                exchanged(ahead - ring).wait_send()

        exchanged(k).wait_recv()
        for h in range(2):
            enter(k, h)
        look_up(0)
        for h in range(2):
            reduce_middle(0, h)
        look_up(1)
        for h in range(2):
            reduce_last(0, h)
        for h in range(2):
            reduce_done(0, h)

            def to_mid(at, value, h=h):
                mid[h, :, at] = value

            cross(0, h, emb, to_mid)
            project(1, h, mid)
        look_up(2)
        for h in range(2):
            reduce_middle(1, h)
        look_up(3)

        @pl.when(more)
        def _():
            send(ahead, pl.ds(0, slots))
            keep(ahead)

        for h in range(2):
            reduce_last(1, h)
        for h in range(2):
            reduce_done(1, h)

            @pl.when(k > 0)
            def _(h=h):
                out_copy(k - 1, h).wait()

            def to_out(at, value, h=h):
                result[h, :, at] = value

            cross(1, h, mid, to_out)
            out_copy(k, h).start()

    for h in range(2):
        out_copy(chunks - 1, h).wait()

    @pl.loop(max(chunks - ring, 0), chunks)
    def _(k):
        exchanged(k).wait_send()


def pipeline(table_feature, bias, ids, tables, cross_down, cross_up, sources, groups):
    slots, buckets, emb_dim = tables.shape
    layers, width, rank = cross_down.shape
    feats = table_feature.shape[0]
    emb_local = emb_dim // groups
    part = LANES
    share = part // 2
    chunks = ids.shape[1] // sources // (2 * part)
    pairs = slots // 2
    blocks = CORES * sources
    dma = pltpu.SemaphoreType.DMA
    bf16, f32 = jnp.bfloat16, jnp.float32
    return pl.pallas_call(
        functools.partial(kernel, sources, groups),
        out_shape=jax.ShapeDtypeStruct((chunks * 2 * part, width), bf16),
        in_specs=[
            pl.BlockSpec(memory_space=pltpu.SMEM),
            pl.BlockSpec(memory_space=pltpu.VMEM),
        ]
        + [pl.BlockSpec(memory_space=pl.ANY)] * 4,
        out_specs=pl.BlockSpec(memory_space=pl.ANY),
        scratch_shapes=[
            pltpu.SMEM((chunks, sources, slots, part), jnp.int32),
            pltpu.VMEM((2, 2, buckets // STEPS, emb_dim), bf16),
            pltpu.VMEM((pairs * buckets, emb_dim), f32),
            pltpu.VMEM((sources * part, emb_dim), f32),
            pltpu.VMEM((min(AHEAD + 1, chunks), blocks, slots, emb_local, part), bf16),
            pltpu.VMEM((chunks, blocks, slots, emb_local, part), bf16),
            pltpu.VMEM((layers, width, rank), bf16),
            pltpu.VMEM((layers, rank, width), bf16),
            pltpu.VMEM((feats * GROUP, feats * GROUP), bf16),
            pltpu.VMEM((2, part, width), bf16),
            pltpu.VMEM((2, part, width), bf16),
            pltpu.VMEM((2, part, width), bf16),
            pltpu.VMEM((layers, 2, part, rank), bf16),
            pltpu.VMEM((layers, 2, share, rank), bf16),
            pltpu.VMEM((layers, 2, share, rank), bf16),
            pltpu.VMEM((layers, 2, share, rank), bf16),
            pltpu.VMEM((layers, 2, part, rank), bf16),
            dma((chunks,)),
            dma((2,)),
            dma((2,)),
            dma((chunks,)),
            dma((chunks,)),
            dma((3, layers, 2)),
            dma((3, layers, 2)),
            dma((2,)),
        ],
        compiler_params=pltpu.CompilerParams(
            collective_id=0, has_side_effects=True, vmem_limit_bytes=LIMIT
        ),
        name="pipeline",
    )(table_feature, bias, ids, tables, cross_down, cross_up)


def finish_kernel(x_ref, out_ref, held, read_sem, write_sem):
    pieces, rows = held.shape[:2]

    def read(i):
        return pltpu.make_async_copy(x_ref.at[pl.ds(i * rows, rows)], held.at[i], read_sem.at[i])

    def write(i):
        return pltpu.make_async_copy(held.at[i], out_ref.at[pl.ds(i * rows, rows)], write_sem.at[i])

    for i in range(pieces):
        read(i).start()
    for i in range(pieces):
        read(i).wait()
        write(i).start()
    for i in range(pieces):
        write(i).wait()


def finish(x):
    rows, width = x.shape
    dma = pltpu.SemaphoreType.DMA
    return pl.pallas_call(
        finish_kernel,
        out_shape=jax.ShapeDtypeStruct(x.shape, x.dtype),
        in_specs=[pl.BlockSpec(memory_space=pl.ANY)],
        out_specs=pl.BlockSpec(memory_space=pl.ANY),
        scratch_shapes=[
            pltpu.VMEM((PIECES, rows // PIECES, width), x.dtype),
            dma((PIECES,)),
            dma((PIECES,)),
        ],
        compiler_params=pltpu.CompilerParams(vmem_limit_bytes=LIMIT),
        name="finish",
    )(x)


def per_device(lookup_ids, table_feature, tables, cross_down, cross_up, cross_bias):
    sources = lax.axis_size("batch")
    groups = lax.axis_size("mp")
    return finish(
        pipeline(
            table_feature, cross_bias, lookup_ids, tables, cross_down, cross_up, sources, groups
        )
    )


def solution(mesh):
    return jax.shard_map(
        per_device,
        mesh=mesh,
        in_specs=(
            P("batch", None),
            P(),
            P("batch", None, None),
            P(None, "mp", None),
            P(None, None, "mp"),
            P(None, "mp"),
        ),
        out_specs=P("batch", "mp"),
        check_vma=False,
    )
```

time: 244 us -> 220 us (0.902)
  Pallas kernels: 234 us -> 219 us
  local copies, waits for them, and re-layouts: 10.2 us -> 0 us
    pallas_call x1, Pallas kernels: 234 us -> 213 us  [pipeline(): pl.pallas_call(functools.partial(kernel, sources, groups), out_shape=jax....]
    unnamed x3 -> x0, local copies, waits for them, and re-layouts: 9.46 us -> none
    pallas_call x0 -> x1, Pallas kernels: none -> 6.57 us  [finish(): pl.pallas_call(finish_kernel, out_shape=jax.ShapeDtypeStruct(x.shape, x.d...]
where the time goes in v2:
time: 220 us; the launch traced here: 219 us
  Pallas kernels  219 us (100%)
    pallas_call x1, Pallas kernels, pipeline(): pl.pallas_call(functools.partial(kernel, sources, groups), out_shape=jax....  213 us
    pallas_call x1, Pallas kernels, finish(): pl.pallas_call(finish_kernel, out_shape=jax.ShapeDtypeStruct(x.shape, x.d...  6.57 us

profile of v2, /device:TPU:0, one launch (start us, length us, event | category | flops | bytes accessed | tf_op | source)
XLA Modules:
  0.0 219.2 jit_solution(6338567397452776973)
XLA Ops:
  0.0 212.7 %pipeline.1.x_ref = bf16[2048,2048]{1,0:T(8,128)(2,1)} custom-call(s32[64]{0:T(128)} %feature_ref.1, f32[2,2048]{1,0:T(2,128)} %bias_ref.1, s32[8,16384]{1,0:T(8,128)} %ids_ref.1, bf16[8,8192,128]{2,1,0:T(8,128)(2,1)} %tables_ref.1, bf16[2,2048,512]{2,1,0:T(8,128)(2,1)} %down_ref.1, bf16[2,512,2048]{2,1,0:T(8,128)(2,1)} %up_ref.1), custom_call_target="tpu_custom_call" | custom-call | tf_op jit(solution)/shard_map/pipeline/pallas_call | solution.py:382
  212.7 6.6 %finish.1 = bf16[2048,2048]{1,0:T(8,128)(2,1)} custom-call(bf16[2048,2048]{1,0:T(8,128)(2,1)} %pipeline.1.x_ref), custom_call_target="tpu_custom_call" | custom-call | tf_op jit(solution)/shard_map/finish/pallas_call | solution.py:446

commit v3 on v2

--- a/solution.py
+++ b/solution.py
@@ -15,7 +15,7 @@
 AHEAD = 3
 PHASES = 4
 STEPS = 4
-PIECES = 16
+PIECES = 8
 LIMIT = 67_043_328
 
 
@@ -232,31 +232,36 @@
     def to_near(layer, h):
         return remote(term.at[layer, h, theirs], near_in.at[layer, h], 0, layer, h, near)
 
-    def to_far(layer, h):
-        return remote(held.at[layer, h], far_in.at[layer, h], 1, layer, h, far)
+    def turn(layer, k):
+        return 2 * layer + k % 2
+
+    def to_far(layer, h, k):
+        slot = turn(layer, k)
+        return remote(held.at[slot, h], far_in.at[slot, h], 1, slot, h, far)
 
     def back(layer, h):
         place = low.at[layer, h, mine]
         return remote(place, place, 2, layer, h, near)
 
-    def reduce_middle(layer, h):
+    def reduce_middle(layer, h, k):
         to_near(layer, h).wait_recv()
-        held[layer, h] = (
+        held[turn(layer, k), h] = (
             term[layer, h, mine].astype(jnp.float32) + near_in[layer, h].astype(jnp.float32)
         ).astype(jnp.bfloat16)
-        to_far(layer, h).start()
-
-    def reduce_last(layer, h):
-        to_far(layer, h).wait_recv()
+        to_far(layer, h, k).start()
+
+    def reduce_last(layer, h, k):
+        slot = turn(layer, k)
+        to_far(layer, h, k).wait_recv()
         low[layer, h, mine] = (
-            held[layer, h].astype(jnp.float32) + far_in[layer, h].astype(jnp.float32)
+            held[slot, h].astype(jnp.float32) + far_in[slot, h].astype(jnp.float32)
         ).astype(jnp.bfloat16)
         back(layer, h).start()
 
-    def reduce_done(layer, h):
+    def reduce_done(layer, h, k):
         back(layer, h).wait_recv()
         to_near(layer, h).wait_send()
-        to_far(layer, h).wait_send()
+        to_far(layer, h, k).wait_send()
         back(layer, h).wait_send()
 
     def project(layer, h, state):
@@ -268,17 +273,17 @@
     def enter(k, h):
         for j in range(emb_local // GROUP):
             x = received[k, h * sources : (h + 1) * sources, :, j * GROUP : (j + 1) * GROUP]
-            emb[h, :, j * cols : (j + 1) * cols] = lax.dot_general(
+            emb[k % 2, h, :, j * cols : (j + 1) * cols] = lax.dot_general(
                 x.reshape(cols, part),
                 placing[...],
                 (((0,), (0,)), ((), ())),
                 preferred_element_type=jnp.float32,
             ).astype(jnp.bfloat16)
-        project(0, h, emb)
+        project(0, h, emb.at[k % 2])
 
     tile = width // TILES
 
-    def cross(layer, h, state, store):
+    def cross(layer, h, first, state, store):
         for n in range(TILES):
             at = slice(n * tile, (n + 1) * tile)
             high = (
@@ -288,13 +293,30 @@
             store(
                 at,
                 (
-                    emb[h, :, at].astype(jnp.float32) * high + state[h, :, at].astype(jnp.float32)
+                    first[h, :, at].astype(jnp.float32) * high
+                    + state[h, :, at].astype(jnp.float32)
                 ).astype(jnp.bfloat16),
             )
 
     def out_copy(k, h):
         span = pl.ds(pl.multiple_of((h * chunks + k) * part, part), part)
         return pltpu.make_async_copy(result.at[h], out_ref.at[span], out_sem.at[h])
+
+    def leave(k):
+        for h in range(2):
+            reduce_last(1, h, k)
+        for h in range(2):
+            reduce_done(1, h, k)
+
+            @pl.when(k > 0)
+            def _(h=h):
+                out_copy(k - 1, h).wait()
+
+            def to_out(at, value, h=h):
+                result[h, :, at] = value
+
+            cross(1, h, emb.at[k % 2], mid, to_out)
+            out_copy(k, h).start()
 
     @pl.loop(0, chunks)
     def _(k):
@@ -322,21 +344,24 @@
             enter(k, h)
         look_up(0)
         for h in range(2):
-            reduce_middle(0, h)
+            reduce_middle(0, h, k)
+
+        @pl.when(k > 0)
+        def _():
+            leave(k - 1)
+
         look_up(1)
-        for h in range(2):
-            reduce_last(0, h)
-        for h in range(2):
-            reduce_done(0, h)
+        look_up(2)
+        for h in range(2):
+            reduce_last(0, h, k)
+        for h in range(2):
+            reduce_done(0, h, k)
 
             def to_mid(at, value, h=h):
                 mid[h, :, at] = value
 
-            cross(0, h, emb, to_mid)
+            cross(0, h, emb.at[k % 2], emb.at[k % 2], to_mid)
             project(1, h, mid)
-        look_up(2)
-        for h in range(2):
-            reduce_middle(1, h)
         look_up(3)
 
         @pl.when(more)
@@ -345,20 +370,9 @@
             keep(ahead)
 
         for h in range(2):
-            reduce_last(1, h)
-        for h in range(2):
-            reduce_done(1, h)
-
-            @pl.when(k > 0)
-            def _(h=h):
-                out_copy(k - 1, h).wait()
-
-            def to_out(at, value, h=h):
-                result[h, :, at] = value
-
-            cross(1, h, mid, to_out)
-            out_copy(k, h).start()
-
+            reduce_middle(1, h, k)
+
+    leave(chunks - 1)
     for h in range(2):
         out_copy(chunks - 1, h).wait()
 
@@ -398,21 +412,21 @@
             pltpu.VMEM((layers, width, rank), bf16),
             pltpu.VMEM((layers, rank, width), bf16),
             pltpu.VMEM((feats * GROUP, feats * GROUP), bf16),
-            pltpu.VMEM((2, part, width), bf16),
+            pltpu.VMEM((2, 2, part, width), bf16),
             pltpu.VMEM((2, part, width), bf16),
             pltpu.VMEM((2, part, width), bf16),
             pltpu.VMEM((layers, 2, part, rank), bf16),
             pltpu.VMEM((layers, 2, share, rank), bf16),
-            pltpu.VMEM((layers, 2, share, rank), bf16),
-            pltpu.VMEM((layers, 2, share, rank), bf16),
+            pltpu.VMEM((2 * layers, 2, share, rank), bf16),
+            pltpu.VMEM((2 * layers, 2, share, rank), bf16),
             pltpu.VMEM((layers, 2, part, rank), bf16),
             dma((chunks,)),
             dma((2,)),
             dma((2,)),
             dma((chunks,)),
             dma((chunks,)),
-            dma((3, layers, 2)),
-            dma((3, layers, 2)),
+            dma((3, 2 * layers, 2)),
+            dma((3, 2 * layers, 2)),
             dma((2,)),
         ],
         compiler_params=pltpu.CompilerParams(

time: 220 us -> 214 us (0.973)
  Pallas kernels: 219 us -> 214 us
    pallas_call x1, Pallas kernels: 213 us -> 207 us  [pipeline(): pl.pallas_call(functools.partial(kernel, sources, groups), out_shape=jax....]
where the time goes in v3:
time: 214 us
  Pallas kernels  214 us (100%)
    pallas_call x1, Pallas kernels, pipeline(): pl.pallas_call(functools.partial(kernel, sources, groups), out_shape=jax....  207 us
    pallas_call x1, Pallas kernels, finish(): pl.pallas_call(finish_kernel, out_shape=jax.ShapeDtypeStruct(x.shape, x.d...  6.42 us

profile of v3, /device:TPU:0, one launch (start us, length us, event | category | flops | bytes accessed | tf_op | source)
XLA Modules:
  0.0 213.9 jit_solution(3571316055384027881)
XLA Ops:
  0.0 207.4 %pipeline.1.x_ref = bf16[2048,2048]{1,0:T(8,128)(2,1)} custom-call(s32[64]{0:T(128)} %feature_ref.1, f32[2,2048]{1,0:T(2,128)} %bias_ref.1, s32[8,16384]{1,0:T(8,128)} %ids_ref.1, bf16[8,8192,128]{2,1,0:T(8,128)(2,1)} %tables_ref.1, bf16[2,2048,512]{2,1,0:T(8,128)(2,1)} %down_ref.1, bf16[2,512,2048]{2,1,0:T(8,128)(2,1)} %up_ref.1), custom_call_target="tpu_custom_call" | custom-call | tf_op jit(solution)/shard_map/pipeline/pallas_call | solution.py:396
  207.4 6.4 %finish.1 = bf16[2048,2048]{1,0:T(8,128)(2,1)} custom-call(bf16[2048,2048]{1,0:T(8,128)(2,1)} %pipeline.1.x_ref), custom_call_target="tpu_custom_call" | custom-call | tf_op jit(solution)/shard_map/finish/pallas_call | solution.py:460

commit v4 on v3

--- a/solution.py
+++ b/solution.py
@@ -270,16 +270,30 @@
         ).astype(jnp.bfloat16)
         to_near(layer, h).start()
 
-    def enter(k, h):
+    def enter(k):
+        first = emb.at[k % 2]
         for j in range(emb_local // GROUP):
-            x = received[k, h * sources : (h + 1) * sources, :, j * GROUP : (j + 1) * GROUP]
-            emb[k % 2, h, :, j * cols : (j + 1) * cols] = lax.dot_general(
-                x.reshape(cols, part),
+            at = slice(j * cols, (j + 1) * cols)
+            sides = [
+                received[
+                    k, h * sources : (h + 1) * sources, :, j * GROUP : (j + 1) * GROUP
+                ].reshape(cols, part)
+                for h in range(2)
+            ]
+            placed = lax.dot_general(
+                jnp.concatenate(sides, axis=1),
                 placing[...],
                 (((0,), (0,)), ((), ())),
                 preferred_element_type=jnp.float32,
             ).astype(jnp.bfloat16)
-        project(0, h, emb.at[k % 2])
+            for h in range(2):
+                first[h, :, at] = placed[h * part : (h + 1) * part]
+        low_part = jnp.dot(
+            first[...].reshape(2 * part, width), down[0], preferred_element_type=jnp.float32
+        ).astype(jnp.bfloat16)
+        for h in range(2):
+            term[0, h] = low_part[h * part : (h + 1) * part]
+            to_near(0, h).start()
 
     tile = width // TILES
 
@@ -340,8 +354,7 @@
                 exchanged(ahead - ring).wait_send()
 
         exchanged(k).wait_recv()
-        for h in range(2):
-            enter(k, h)
+        enter(k)
         look_up(0)
         for h in range(2):
             reduce_middle(0, h, k)

time: 214 us -> 215 us (level)
  no operation moved by 1% of the time
where the time goes in v4:
time: 215 us
  Pallas kernels  215 us (100%)
    pallas_call x1, Pallas kernels, pipeline(): pl.pallas_call(functools.partial(kernel, sources, groups), out_shape=jax....  208 us
    pallas_call x1, Pallas kernels, finish(): pl.pallas_call(finish_kernel, out_shape=jax.ShapeDtypeStruct(x.shape, x.d...  6.42 us

profile of v4, /device:TPU:0, one launch (start us, length us, event | category | flops | bytes accessed | tf_op | source)
XLA Modules:
  0.0 214.6 jit_solution(8319544227017247725)
XLA Ops:
  0.0 208.2 %pipeline.1.x_ref = bf16[2048,2048]{1,0:T(8,128)(2,1)} custom-call(s32[64]{0:T(128)} %feature_ref.1, f32[2,2048]{1,0:T(2,128)} %bias_ref.1, s32[8,16384]{1,0:T(8,128)} %ids_ref.1, bf16[8,8192,128]{2,1,0:T(8,128)(2,1)} %tables_ref.1, bf16[2,2048,512]{2,1,0:T(8,128)(2,1)} %down_ref.1, bf16[2,512,2048]{2,1,0:T(8,128)(2,1)} %up_ref.1), custom_call_target="tpu_custom_call" | custom-call | tf_op jit(solution)/shard_map/pipeline/pallas_call | solution.py:409
  208.2 6.4 %finish.1 = bf16[2048,2048]{1,0:T(8,128)(2,1)} custom-call(bf16[2048,2048]{1,0:T(8,128)(2,1)} %pipeline.1.x_ref), custom_call_target="tpu_custom_call" | custom-call | tf_op jit(solution)/shard_map/finish/pallas_call | solution.py:473
